TPU v7x, 128 devices: a whole 4x4x4 slice. The times are simulated.
128 devices in a mesh: dp: 1, ep: 128 (over z, y, x, core).
Axes of the slice: x: 4, y: 4, z: 4, core: 2. Of those that a mesh axis runs over, the one named last changes fastest.
Arguments:
- tokens: bfloat16 [32768, 2048], P(('dp', 'ep'))
- routes: int32 [32768, 8], P(('dp', 'ep'))
- w_router: bfloat16 [2048, 128], replicated
- w_one: bfloat16 [128, 2048, 768], P('ep')
- w_three: bfloat16 [128, 2048, 768], P('ep')
- w_two: bfloat16 [128, 768, 2048], P('ep')
Outputs:
- output: bfloat16 [32768, 2048], P(('dp', 'ep'))
All inputs are finite; a program needn't handle non-finite values.
Results may differ from a plain program's by a relative error of at most 0.00819171.
Values are sent between devices in bfloat16 or wider.
A program may use at most 1 GiB of HBM per device.

v0:
```python
import jax
import jax.numpy as jnp
from jax import lax
from jax.sharding import PartitionSpec as P


def slot_capacity(num_tokens, top_k, num_experts):
    return 8 * ((3 * num_tokens * top_k + 16 * num_experts - 1) // (16 * num_experts))


def route_gates(tokens, routes, w_router):
    logits = jnp.dot(tokens, w_router, preferred_element_type=jnp.float32)
    return jax.nn.softmax(jnp.take_along_axis(logits, routes, axis=1), axis=-1)


def dispatch_plan(routes, num_experts, capacity):
    top_k = routes.shape[1]
    flat_routes = routes.reshape(-1)
    num_pairs = flat_routes.shape[0]
    sort_order = jnp.argsort(flat_routes, stable=True)
    counts = jax.ops.segment_sum(jnp.ones_like(flat_routes), flat_routes, num_segments=num_experts)
    starts = jnp.cumsum(counts) - counts
    slot_ids = starts[:, None] + jnp.arange(capacity, dtype=jnp.int32)[None, :]
    token_at = sort_order[jnp.minimum(slot_ids, num_pairs - 1)] // top_k
    pair_rank = jnp.zeros_like(sort_order).at[sort_order].set(jnp.arange(num_pairs, dtype=sort_order.dtype))
    pair_row = flat_routes * capacity + pair_rank - starts[flat_routes]
    return token_at, pair_row


def expert_mlp(rows, w_one, w_three, w_two):
    gate_pre = jnp.einsum('erd,edf->erf', rows, w_one, preferred_element_type=jnp.float32)
    up_pre = jnp.einsum('erd,edf->erf', rows, w_three, preferred_element_type=jnp.float32)
    hidden = (jax.nn.silu(gate_pre) * up_pre).astype(jnp.bfloat16)
    return jnp.einsum('erf,efd->erd', hidden, w_two, preferred_element_type=jnp.float32).astype(jnp.bfloat16)


def solution(mesh):
    group_size = mesh.shape['ep']
    row_spec = P(('dp', 'ep'), None)
    expert_spec = P('ep', None, None)

    def device_step(tokens, routes, w_router, w_one, w_three, w_two):
        num_tokens, d_model = tokens.shape
        top_k = routes.shape[1]
        num_experts = w_router.shape[1]
        local_experts = w_one.shape[0]
        capacity = slot_capacity(num_tokens, top_k, num_experts)
        gate_vals = route_gates(tokens, routes, w_router)
        token_at, pair_row = dispatch_plan(routes, num_experts, capacity)
        send_rows = tokens[token_at].reshape(num_experts, 1, capacity, d_model)
        recv_rows = lax.all_to_all(send_rows, 'ep', 0, 1, tiled=True)
        out_rows = expert_mlp(recv_rows.reshape(local_experts, group_size * capacity, d_model), w_one, w_three, w_two)
        back_rows = lax.all_to_all(out_rows.reshape(local_experts, group_size, capacity, d_model), 'ep', 1, 0, tiled=True)
        pair_out = back_rows.reshape(num_experts * capacity, d_model)[pair_row].reshape(num_tokens, top_k, d_model)
        return jnp.sum(gate_vals[:, :, None] * pair_out, axis=1).astype(jnp.bfloat16)

    return jax.shard_map(device_step, mesh=mesh, in_specs=(row_spec, row_spec, P(None, None), expert_spec, expert_spec, expert_spec), out_specs=row_spec, check_vma=False)
```

profile of v0, /device:TPU:0, one launch (start us, length us, event | category | flops | bytes accessed | tf_op | source)
XLA Modules:
  0.0 510.6 jit_solution(13647730468107150823)
XLA Ops:
  0.0 0.0 copy-start
  0.0 1.0 copy.30
  1.0 0.1 reshape.238
  1.1 0.0 copy-start.6
  1.1 5.0 sort.17
  6.2 14.7 %scatter_custom_fusion = s32[128]{0:T(128)S(1)} fusion(s32[2048]{0:T(1024)S(1)} %reshape.238, s32[2048]{0:T(1024)S(1)} %broadcast.170, s32[]{:T(128)} %constant.17.clone.1), kind=kCustom, calls=%fused_computation.39 | custom fusion | flops 2048 | bytes 516 | tf_op jit(solution)/shard_map/scatter-add | solution.py:21
  20.8 0.0 copy-done.6
  20.8 0.1 copy.31
  20.9 0.2 reduce-window.9
  21.1 0.1 reduce
  21.2 0.1 compare_select_fusion.1
  21.3 0.1 reshape.251
  21.4 17.4 %gather_fusion = s32[3072]{0:T(1024)S(1)} fusion(s32[2048]{0:T(1024)S(1)} %get-tuple-element.6, s32[3072]{0:T(1024)S(1)} %broadcast_clamp_fusion.1), kind=kCustom, calls=%fused_computation | custom fusion | bytes 36864 | tf_op jit(solution)/shard_map/gather | solution.py:24
  38.9 0.1 gather.20
  39.0 0.1 reshape.259
  39.1 25.2 %gather_fusion.1 = bf16[3072,2048]{1,0:T(8,128)(2,1)} fusion(bf16[256,2048]{1,0:T(8,128)(2,1)} %param.6, s32[3072]{0:T(1024)S(1)} %broadcast_clamp_fusion), kind=kCustom, calls=%fused_computation.1 | custom fusion | bytes 25178112 | tf_op jit(solution)/shard_map/gather | solution.py:50
  64.3 0.0 copy-start.8
  64.3 181.1 %all_to_all.8 = bf16[128,1,24,2048]{3,2,1,0:T(8,128)(2,1)S(1)} all-to-all(bf16[128,1,24,2048]{3,2,1,0:T(8,128)(2,1)} %bitcast.36), channel_id=1, replica_groups=mesh['dp'=1,'ep'=128] {'ep'}, dimensions={0} | all-to-all | bytes 25165824 | tf_op jit(solution)/shard_map/all_to_all | solution.py:51
  245.4 0.0 copy-start.3
  245.4 4.5 copy-done.3
  249.8 0.0 copy-done.8
  249.8 12.5 %fusion.4 = f32[3072,768]{1,0:T(8,128)} fusion(bf16[3072,2048]{1,0:T(8,128)(2,1)S(1)} %bitcast.38, bf16[1,2048,768]{2,1,0:T(8,128)(2,1)S(1)} %copy-done.8), kind=kOutput, calls=%fused_computation.13 | convolution fusion | flops 9663676416 | bytes 25165824 | tf_op jit(solution)/shard_map/erd,edf->erf/dot_general | solution.py:31
  262.3 0.0 copy-done
  262.3 28.9 %convolution_convert_fusion = bf16[3072,2048]{1,0:T(8,128)(2,1)} fusion(f32[3072,768]{1,0:T(8,128)} %fusion.4, bf16[3072,2048]{1,0:T(8,128)(2,1)} %bitcast.39, bf16[1,768,2048]{2,1,0:T(8,128)(2,1)S(1)} %copy-done, bf16[1,2048,768]{2,1,0:T(8,128)(2,1)} %param.10), kind=kOutput, calls=%fused_computation.9 | convolution fusion | flops 19347800064 | bytes 40894464 | tf_op jit(solution)/shard_map/erf,efd->erd/dot_general | solution.py:34
  291.2 0.0 copy-start.5
  291.2 0.0 copy-start.2
  291.2 0.0 copy-start.4
  291.2 14.6 %all-to-all-start.1 = ((bf16[1,128,24,2048]{3,2,0,1:T(8,128)(2,1)}), bf16[1,128,24,2048]{3,2,0,1:T(8,128)(2,1)}, u32[]{:S(2)}, u32[]{:S(2)}) async-start(bf16[1,128,24,2048]{3,2,0,1:T(8,128)(2,1)} %bitcast.37), calls=%async_computation.1 | async-start | bytes 25165824 | tf_op jit(solution)/shard_map/all_to_all | solution.py:53
  305.8 0.1 broadcast_in_dim_reshape.3
  305.9 0.0 copy-done.5
  305.9 0.1 copy.27
  306.1 0.1 reshape.281
  306.2 12.6 %gather_fusion.2 = s32[2048]{0:T(1024)S(1)} fusion(s32[128]{0:T(128)S(1)} %sub.24, s32[2048]{0:T(1024)S(1)} %broadcast_clamp_fusion.2), kind=kCustom, calls=%fused_computation.2 | custom fusion | bytes 24576 | tf_op jit(solution)/shard_map/gather | solution.py:26
  318.8 0.0 copy-done.2
  318.9 0.0 copy-done.4
  318.9 0.4 fusion.17
  319.3 0.0 copy-start.7
  319.3 13.1 %gather_fusion.4 = f32[2048]{0:T(1024)S(1)} fusion(f32[256,128]{1,0:T(8,128)S(1)} %fusion.17, s32[2048]{0:T(1024)S(1)} %reshape.281), kind=kCustom, calls=%fused_computation.4 | custom fusion | bytes 32768 | tf_op jit(solution)/shard_map/jit(take_along_axis)/gather | solution.py:13
  332.4 0.1 reshape.284
  332.5 0.1 copy.28
  332.6 0.1 copy.29
  332.8 8.3 %scatter_custom_fusion.1 = s32[2048]{0:T(1024)S(1)} fusion(s32[2048]{0:T(1024)S(1)} %compare_select_fusion.4, s32[2048]{0:T(1024)S(1)} %iota.14, s32[]{:T(128)} %constant.17.clone.1), kind=kCustom, calls=%fused_computation.37 | custom fusion | bytes 8196 | tf_op jit(solution)/shard_map/scatter | solution.py:25
  341.1 0.0 copy-done.7
  341.1 134.6 %all-to-all-done.1 = bf16[1,128,24,2048]{3,2,0,1:T(8,128)(2,1)} async-done(((bf16[1,128,24,2048]{3,2,0,1:T(8,128)(2,1)}), bf16[1,128,24,2048]{3,2,0,1:T(8,128)(2,1)}, u32[]{:S(2)}, u32[]{:S(2)}) %all-to-all-start.1) | async-done | bytes 12582944 | tf_op jit(solution)/shard_map/all_to_all | solution.py:53
  475.7 0.0 copy-start.1
  475.7 22.7 %gather_fusion.3 = bf16[2048,2048]{1,0:T(8,128)(2,1)} fusion(bf16[3072,2048]{1,0:T(8,128)(2,1)} %bitcast.10, s32[2048]{0:T(1024)S(1)} %fusion.8), kind=kCustom, calls=%fused_computation.3 | custom fusion | bytes 16785408 | tf_op jit(solution)/shard_map/gather | solution.py:54
  498.3 12.3 %fusion = bf16[256,2048]{1,0:T(8,128)(2,1)} fusion(bf16[2048,2048]{1,0:T(8,128)(2,1)} %gather_fusion.3, f32[256,8]{1,0:T(8,128)S(1)} %copy.29), kind=kLoop, calls=%fused_computation.8 | loop fusion | flops 12058624 | bytes 9445376 | tf_op jit(solution)/shard_map/reduce_sum | solution.py:55
  510.6 0.0 copy-done.1
  (15 shorter events, 0.2 us)
Async XLA Ops:
  0.0 262.3 %copy-start = (bf16[1,768,2048]{2,1,0:T(8,128)(2,1)S(1)}, bf16[1,768,2048]{2,1,0:T(8,128)(2,1)}, u32[]{:S(2)}) copy-start(bf16[1,768,2048]{2,1,0:T(8,128)(2,1)} %param.11) | copy-start | bytes 9437188
  1.1 19.7 %copy-start.6 = (s32[2048]{0:T(1024)}, s32[2048]{0:T(1024)S(1)}, u32[]{:S(2)}) copy-start(s32[2048]{0:T(1024)S(1)} %reshape.238) | copy-start | bytes 24580
  64.3 185.5 %copy-start.8 = (bf16[1,2048,768]{2,1,0:T(8,128)(2,1)S(1)}, bf16[1,2048,768]{2,1,0:T(8,128)(2,1)}, u32[]{:S(2)}) copy-start(bf16[1,2048,768]{2,1,0:T(8,128)(2,1)} %param.9) | copy-start | bytes 9437188
  245.4 4.5 copy-start.3
  291.2 14.7 %copy-start.5 = (s32[256,8]{0,1:T(8,128)S(1)}, s32[256,8]{0,1:T(8,128)}, u32[]{:S(2)}) copy-start(s32[256,8]{0,1:T(8,128)} %param.7) | copy-start | bytes 24580
  291.2 27.6 %copy-start.2 = (bf16[256,2048]{1,0:T(8,128)(2,1)S(1)}, bf16[256,2048]{1,0:T(8,128)(2,1)}, u32[]{:S(2)}) copy-start(bf16[256,2048]{1,0:T(8,128)(2,1)} %param.6) | copy-start | bytes 3145732
  291.2 27.6 %copy-start.4 = (bf16[2048,128]{1,0:T(8,128)(2,1)S(1)}, bf16[2048,128]{1,0:T(8,128)(2,1)}, u32[]{:S(2)}) copy-start(bf16[2048,128]{1,0:T(8,128)(2,1)} %param.8) | copy-start | bytes 1572868
  291.2 184.4 %all-to-all-start.1 = ((bf16[1,128,24,2048]{3,2,0,1:T(8,128)(2,1)}), bf16[1,128,24,2048]{3,2,0,1:T(8,128)(2,1)}, u32[]{:S(2)}, u32[]{:S(2)}) async-start(bf16[1,128,24,2048]{3,2,0,1:T(8,128)(2,1)} %bitcast.37), calls=%async_computation.1 | async-start | bytes 25165824 | tf_op jit(solution)/shard_map/all_to_all | solution.py:53
  319.3 21.8 %copy-start.7 = (s32[2048]{0:T(1024)S(1)}, s32[2048]{0:T(1024)}, u32[]{:S(2)}) copy-start(s32[2048]{0:T(1024)} %copy-done.6) | copy-start | bytes 24580
  475.7 34.9 %copy-start.1 = (bf16[1,768,2048]{2,1,0:T(8,128)(2,1)S(1)}, bf16[1,768,2048]{2,1,0:T(8,128)(2,1)}, u32[]{:S(2)}) copy-start(bf16[1,768,2048]{2,1,0:T(8,128)(2,1)} %param.11) | copy-start | bytes 9437188
where the time goes:
time: 514 us; the launch traced here: 511 us
  blocking collectives  181 us (35%)
  waiting for transfers between devices  135 us (26%)
  local copies, waits for them, and re-layouts  106 us (21%)
  matrix products  41.8 us (8%)
  other arithmetic  32.5 us (6%)
  starting transfers between devices  14.6 us (3%)
    all_to_all x1, blocking collectives, device_step(): recv_rows = lax.all_to_all(send_rows, 'ep', 0, 1, tiled=True)  181 us
    all_to_all x1, waiting for transfers between devices, device_step(): lax.all_to_all(out_rows.reshape(local_experts, group_size, capacity, d_mo...  135 us
    dot_general x1, matrix products, expert_mlp(): jnp.einsum('erf,efd->erd', hidden, w_two, preferred_element_type=jnp.floa...  28.9 us
    gather x1, local copies, waits for them, and re-layouts, device_step(): send_rows = tokens[token_at].reshape(num_experts, 1, capacity, d_model)  25.2 us
    gather x1, local copies, waits for them, and re-layouts, device_step(): back_rows.reshape(num_experts * capacity, d_model)[pair_row]  22.7 us
    gather x2, local copies, waits for them, and re-layouts, dispatch_plan(): token_at = sort_order[jnp.minimum(slot_ids, num_pairs - 1)] // top_k  17.5 us
    scatter-add x1, other arithmetic, dispatch_plan(): jax.ops.segment_sum(jnp.ones_like(flat_routes), flat_routes, num_segments...  14.7 us
    all_to_all x1, starting transfers between devices, device_step(): lax.all_to_all(out_rows.reshape(local_experts, group_size, capacity, d_mo...  14.6 us
  transfers between devices with their start and end apart: 1, of which 1 were waited for; matrix products, arithmetic and copies ran while one was open for 7% of the time, Pallas kernels for 0%

commit v1 on v0

v1 whole, which is shorter than its diff:
```python
import functools

import jax
import jax.numpy as jnp
from jax import lax
from jax.experimental import pallas as pl
from jax.experimental.pallas import tpu as pltpu
from jax.sharding import PartitionSpec as P

MESH = pl.DeviceIdType.MESH
Z, Y, X = 0, 1, 2
ORDERS = ((Z, Y, X), (X, Z, Y), (Y, X, Z))
SLOTS = 8


def slot_capacity(num_tokens, top_k, num_experts):
    return 8 * ((3 * num_tokens * top_k + 16 * num_experts - 1) // (16 * num_experts))


def torus_side(group_size):
    side = 1
    while 2 * side ** 3 < group_size:
        side += 1
    return side


def column_groups(d_model):
    lanes = d_model // 128
    widths = [128 * (lanes // 3 + (1 if i < lanes % 3 else 0)) for i in range(3)]
    starts = [sum(widths[:i]) for i in range(3)]
    return list(zip(starts, widths))


def moved(me, side, axis, steps, core_steps=0):
    digits = [me // (2 * side * side), (me // (2 * side)) % side, (me // 2) % side]
    digits[axis] = (digits[axis] + steps + side) % side
    return ((digits[Z] * side + digits[Y]) * side + digits[X]) * 2 + (me + core_steps) % 2


def route_plan(tokens, routes, w_router, expert_at):
    num_tokens = tokens.shape[0]
    num_experts = w_router.shape[1]
    logits = jnp.dot(tokens, w_router, preferred_element_type=jnp.float32)
    expert_ids = jnp.arange(num_experts, dtype=jnp.int32)
    hits = routes[:, :, None] == expert_ids[None, None, :]
    picked = jnp.sum(jnp.where(hits, logits[:, None, :], 0.0), axis=2)
    gate_vals = jax.nn.softmax(picked, axis=-1)
    routes_t = routes.T
    gates_t = gate_vals.T
    at = routes_t[:, None, :] == expert_at[None, :, None]
    mask_t = jnp.any(at, axis=0)
    gate_t = jnp.sum(jnp.where(at, gates_t[:, None, :], 0.0), axis=0)
    token_ids = jnp.arange(num_tokens, dtype=jnp.int32)
    before = (token_ids[:, None] < token_ids[None, :]).astype(jnp.bfloat16)
    rank_t = jnp.dot(mask_t.astype(jnp.bfloat16), before, preferred_element_type=jnp.float32)
    return jnp.where(mask_t, rank_t, -1.0), gate_t


def moe_kernel(side, chunks, groups, tokens_hbm, plans_hbm, w_one_hbm, w_three_hbm, w_two_hbm, y_own, y_peers,
               toks, plans, packed, relay, rows, w_one, w_three, w_two, parts,
               load_sem, w_sem, s0_sem, r0_sem, sp_sem, rp_sem, s1_sem, r1_sem, s2_sem, r2_sem, b1_sem, c1_sem, b2_sem, c2_sem, s3_sem, r3_sem, out_sem, free2_sem, free3_sem):
    me = lax.axis_index('ep')
    dp = lax.axis_index('dp')
    num_tokens = tokens_hbm.shape[0]
    plane = 2 * side * side
    ends = 2 * side
    packed_rows = plane * SLOTS

    def remote(src, dst, s_sem, r_sem, axis, steps, core_steps=0):
        return pltpu.make_async_remote_copy(
            src_ref=src, dst_ref=dst, send_sem=s_sem, recv_sem=r_sem,
            device_id=(dp, moved(me, side, axis, steps, core_steps)), device_id_type=MESH)

    def columns(g):
        return pl.ds(*groups[g])

    def relay_from(g, q, b):
        return relay[g].at[q, b] if g == 1 else relay[g].at[q, :, b]

    def relay_others(g, q):
        return relay[g].at[q, pl.ds(1, side - 1)] if g == 1 else relay[g].at[q, :, pl.ds(1, side - 1)]

    def rows_at(g, q, e):
        c, core = e // 2, e % 2
        third = ORDERS[g][2]
        where = {Z: (q, c, slice(None), slice(None), core), Y: (q, slice(None), c, slice(None), core),
                 X: (q, slice(None), slice(None), c, core)}[third]
        return where + (slice(None), columns(g))

    def gather_copies(g, a):
        first = ORDERS[g][0]
        return (remote(tokens_hbm.at[:, columns(g)], toks[g].at[a], s0_sem.at[g], r0_sem.at[g], first, a),
                remote(plans_hbm[g].at[a], plans[g].at[a], sp_sem.at[g], rp_sem.at[g], first, a))

    def gather_all(g):
        first = ORDERS[g][0]
        others = pl.ds(1, side - 1)
        return (remote(toks[g].at[others], toks[g].at[others], s0_sem.at[g], r0_sem.at[g], first, 1),
                remote(plans[g].at[others], plans[g].at[others], sp_sem.at[g], rp_sem.at[g], first, 1))

    def out_second(g, q, b):
        return remote(packed[g].at[q, b], relay_from(g, q, b), s1_sem.at[g, q], r1_sem.at[g, q], ORDERS[g][1], b)

    def out_second_all(g, q):
        return remote(packed[g].at[q, pl.ds(1, side - 1)], relay_others(g, q), s1_sem.at[g, q], r1_sem.at[g, q], ORDERS[g][1], 1)

    def out_third(g, q, e):
        return remote(relay[g].at[q, :, :, e], rows.at[rows_at(g, q, e)], s2_sem.at[g, q], r2_sem.at[g, q], ORDERS[g][2], e // 2, e % 2)

    def third_all(g, q, s_sem, r_sem):
        some = relay[g].at[q, :, :, pl.ds(1, ends - 1)]
        return remote(some, some, s_sem.at[g, q], r_sem.at[g, q], ORDERS[g][2], 1)

    def home_third(g, q, e):
        return remote(rows.at[rows_at(g, q, e)], relay[g].at[q, :, :, e], b1_sem.at[g, q], c1_sem.at[g, q], ORDERS[g][2], -(e // 2), e % 2)

    def home_second(g, q, b):
        return remote(relay_from(g, q, b), packed[g].at[q, b], b2_sem.at[g, q], c2_sem.at[g, q], ORDERS[g][1], -b)

    def home_second_all(g, q):
        return remote(relay_others(g, q), packed[g].at[q, pl.ds(1, side - 1)], b2_sem.at[g, q], c2_sem.at[g, q], ORDERS[g][1], 1)

    def home_first(g, a):
        return remote(parts.at[a, :, columns(g)], y_peers.at[a - 1, :, columns(g)], s3_sem.at[g], r3_sem.at[g], ORDERS[g][0], -a)

    def home_first_all(g):
        return remote(parts.at[pl.ds(1, side - 1), :, columns(g)], y_peers.at[:, :, columns(g)], s3_sem.at[g], r3_sem.at[g], ORDERS[g][0], 1)

    def tell(sem, axis, steps, core_steps=0):
        pl.semaphore_signal(sem, inc=1, device_id=(dp, moved(me, side, axis, steps, core_steps)), device_id_type=MESH)

    loads = []
    for g in range(3):
        loads.append((pltpu.make_async_copy(tokens_hbm.at[:, columns(g)], toks[g].at[0], load_sem.at[2 * g]),
                      pltpu.make_async_copy(plans_hbm[g].at[0], plans[g].at[0], load_sem.at[2 * g + 1])))
    weights = [pltpu.make_async_copy(src, dst, w_sem.at[i]) for i, (src, dst) in enumerate(
        [(w_one_hbm, w_one), (w_three_hbm, w_three), (w_two_hbm, w_two)])]

    for a in range(1, side):
        for g in range(3):
            for copy in gather_copies(g, a)[::-1]:
                copy.start()
    for g in range(3):
        for copy in loads[g]:
            copy.start()
    for copy in weights:
        copy.start()
    parts[...] = jnp.zeros_like(parts)

    def taken(g, q, a):
        slots = plans[g][a, pl.ds(0, plane), :]
        ids = lax.broadcasted_iota(jnp.int32, (plane, SLOTS, num_tokens), 1) + q * SLOTS
        return jnp.broadcast_to(slots[:, None, :], (plane, SLOTS, num_tokens)) == ids.astype(jnp.float32)

    for g in range(3):
        for copy in loads[g]:
            copy.wait()
        for copy in gather_all(g):
            copy.wait_recv()

    def pack(q, carry):
        for g in range(3):
            width = groups[g][1]

            def source(a, c):
                select = jnp.where(taken(g, q, a), 1.0, 0.0).reshape(packed_rows, num_tokens).astype(jnp.bfloat16)
                out = jnp.dot(select, toks[g][a], preferred_element_type=jnp.float32)
                packed[g][q, :, a] = out.reshape(side, ends, SLOTS, width).astype(jnp.bfloat16)
                return c
            lax.fori_loop(0, side, source, 0)
            for b in range(1, side):
                out_second(g, q, b).start()
            relay_from(g, q, 0)[...] = packed[g][q, 0]
        return carry

    lax.fori_loop(0, chunks, pack, 0)

    def forward(q, carry):
        for g in range(3):
            out_second_all(g, q).wait_recv()
            for e in range(1, ends):
                out_third(g, q, e).start()
            rows[rows_at(g, q, 0)] = relay[g][q, :, :, 0]
            out_second_all(g, q).wait_send()
            for b in range(1, side):
                tell(free2_sem.at[g, q], ORDERS[g][1], b)
        return carry

    lax.fori_loop(0, chunks, forward, 0)
    for copy in weights:
        copy.wait()

    def experts(q, carry):
        for g in range(3):
            third_all(g, q, s2_sem, r2_sem).wait_recv()
        for g in range(3):
            third_all(g, q, s2_sem, r2_sem).wait_send()
            for e in range(1, ends):
                tell(free3_sem.at[g, q], ORDERS[g][2], e // 2, e % 2)

        def block(z, c):
            shape = rows.shape[2:]
            u = rows[q, z].astype(jnp.float32).reshape(packed_rows, shape[-1]).astype(jnp.bfloat16)
            gate_pre = jnp.dot(u, w_one[...], preferred_element_type=jnp.float32)
            up_pre = jnp.dot(u, w_three[...], preferred_element_type=jnp.float32)
            hidden = (jax.nn.silu(gate_pre) * up_pre).astype(jnp.bfloat16)
            out = jnp.dot(hidden, w_two[...], preferred_element_type=jnp.float32)
            rows[q, z] = out.reshape(shape).astype(jnp.bfloat16)
            return c
        lax.fori_loop(0, side, block, 0)
        for g in range(3):
            pl.semaphore_wait(free3_sem.at[g, q], ends - 1)
            for e in range(1, ends):
                home_third(g, q, e).start()
            relay[g][q, :, :, 0] = rows[rows_at(g, q, 0)]
        return carry

    lax.fori_loop(0, chunks, experts, 0)

    def backward(q, carry):
        for g in range(3):
            third_all(g, q, b1_sem, c1_sem).wait_recv()
            pl.semaphore_wait(free2_sem.at[g, q], side - 1)
            for b in range(1, side):
                home_second(g, q, b).start()
            packed[g][q, 0] = relay_from(g, q, 0)[...]
        return carry

    lax.fori_loop(0, chunks, backward, 0)

    def combine(q, carry):
        for g in range(3):
            home_second_all(g, q).wait_recv()
            width = groups[g][1]

            def source(a, c):
                gates = plans[g][a, pl.ds(plane, plane), :]
                used = taken(g, q, a)
                o = packed[g][q, :, a].astype(jnp.float32).reshape(packed_rows, width).astype(jnp.bfloat16)
                total = None
                for _ in range(3):
                    part = gates.astype(jnp.bfloat16).astype(jnp.float32)
                    gates = gates - part
                    mix = jnp.where(used, jnp.broadcast_to(part[:, None, :], used.shape), 0.0).reshape(packed_rows, num_tokens).astype(jnp.bfloat16)
                    term = lax.dot_general(mix, o, (((0,), (0,)), ((), ())), preferred_element_type=jnp.float32)
                    total = term if total is None else total + term
                parts[a, :, columns(g)] += total
                return c
            lax.fori_loop(0, side, source, 0)

            @pl.when(q == chunks - 1)
            def _():
                for a in range(1, side):
                    home_first(g, a).start()
        return carry

    lax.fori_loop(0, chunks, combine, 0)
    own = pltpu.make_async_copy(parts.at[0], y_own, out_sem)
    own.start()

    for g in range(3):
        for copy in gather_all(g):
            copy.wait_send()

        def drain(q, c):
            third_all(g, q, b1_sem, c1_sem).wait_send()
            home_second_all(g, q).wait_send()
            return c
        lax.fori_loop(0, chunks, drain, 0)
        home_first_all(g).wait_send()
        home_first_all(g).wait_recv()
    own.wait()


def solution(mesh):
    group_size = mesh.shape['ep']
    side = torus_side(group_size)
    row_spec = P(('dp', 'ep'), None)
    expert_spec = P('ep', None, None)

    def device_step(tokens, routes, w_router, w_one, w_three, w_two):
        num_tokens, d_model = tokens.shape
        top_k = routes.shape[1]
        num_experts = w_router.shape[1]
        d_expert = w_one.shape[2]
        capacity = slot_capacity(num_tokens, top_k, num_experts)
        chunks = capacity // SLOTS
        groups = column_groups(d_model)
        plane = 2 * side * side
        me = lax.axis_index('ep')
        position = jnp.arange(num_experts, dtype=jnp.int32)
        expert_at = moved(me, side, Z, position // plane)
        expert_at = moved(expert_at, side, Y, (position // (2 * side)) % side)
        expert_at = moved(expert_at, side, X, (position // 2) % side, position % 2)
        slot_t, gate_t = route_plan(tokens, routes, w_router, expert_at)
        plan = jnp.stack([slot_t, gate_t]).reshape(2, side, side, side, 2, num_tokens)
        plans = []
        for first, second, third in ORDERS:
            ordered = jnp.transpose(plan, (1 + first, 0, 1 + second, 1 + third, 4, 5))
            plans.append(ordered.reshape(side, 2 * plane, num_tokens))
        hbm = pl.BlockSpec(memory_space=pl.ANY)
        dma = pltpu.SemaphoreType.DMA
        slab = [[pltpu.VMEM((chunks, side, side, 2 * side, SLOTS, width), jnp.bfloat16) for _, width in groups] for _ in range(2)]
        pair = [dma((3, chunks)), dma((3, chunks))]
        y_own, y_peers = pl.pallas_call(
            functools.partial(moe_kernel, side, chunks, groups),
            out_shape=(jax.ShapeDtypeStruct((num_tokens, d_model), jnp.float32),
                       jax.ShapeDtypeStruct((side - 1, num_tokens, d_model), jnp.float32)),
            in_specs=[hbm, (hbm, hbm, hbm), hbm, hbm, hbm],
            out_specs=(hbm, hbm),
            scratch_shapes=[
                [pltpu.VMEM((side, num_tokens, width), jnp.bfloat16) for _, width in groups],
                [pltpu.VMEM((side, 2 * plane, num_tokens), jnp.float32) for _ in groups],
                slab[0], slab[1],
                pltpu.VMEM((chunks, side, side, side, 2, SLOTS, d_model), jnp.bfloat16),
                pltpu.VMEM((d_model, d_expert), jnp.bfloat16),
                pltpu.VMEM((d_model, d_expert), jnp.bfloat16),
                pltpu.VMEM((d_expert, d_model), jnp.bfloat16),
                pltpu.VMEM((side, num_tokens, d_model), jnp.float32),
                dma((6,)), dma((3,)), dma((3,)), dma((3,)), dma((3,)), dma((3,)),
                *pair, *pair, *pair, *pair, dma((3,)), dma((3,)), dma,
                pltpu.SemaphoreType.REGULAR((3, chunks)), pltpu.SemaphoreType.REGULAR((3, chunks)),
            ],
            compiler_params=pltpu.CompilerParams(has_side_effects=True, vmem_limit_bytes=67043328),
            name='moe',
        )(tokens, tuple(plans), w_one[0], w_three[0], w_two[0])
        total = y_own
        for i in range(side - 1):
            total = total + y_peers[i]
        return total.astype(jnp.bfloat16)

    return jax.shard_map(device_step, mesh=mesh, in_specs=(row_spec, row_spec, P(None, None), expert_spec, expert_spec, expert_spec), out_specs=row_spec, check_vma=False)
```

time: 514 us -> 273 us (0.53)
  Pallas kernels: 0 us -> 260 us
  blocking collectives: 181 us -> 0 us
  waiting for transfers between devices: 135 us -> 0 us
  local copies, waits for them, and re-layouts: 106 us -> 3.13 us
  matrix products: 41.8 us -> 1.95 us
  other arithmetic: 32.5 us -> 7.27 us
  starting transfers between devices: 14.6 us -> 0 us
    pallas_call x0 -> x1, Pallas kernels: none -> 260 us  [device_step(): pl.pallas_call(functools.partial(moe_kernel, side, chunks, groups), out_s...]
    all_to_all x1 -> x0, blocking collectives: 181 us -> none  [device_step(): recv_rows = lax.all_to_all(send_rows, 'ep', 0, 1, tiled=True)]
    all_to_all x1 -> x0, waiting for transfers between devices: 135 us -> none  [device_step(): lax.all_to_all(out_rows.reshape(local_experts, group_size, capacity, d_mo...]
    gather x10 -> x0, local copies, waits for them, and re-layouts: 91.4 us -> none  [the longest x1 25.2 us: device_step(): send_rows = tokens[token_at].reshape(num_experts, 1, capacity, d_model)]
    dot_general x3 -> x2, matrix products: 41.8 us -> 1.95 us  [the longest x1 1.78 us: route_plan(): logits = jnp.dot(tokens, w_router, preferred_element_type=jnp.float32)]
    scatter-add x1 -> x0, other arithmetic: 14.7 us -> none  [dispatch_plan(): jax.ops.segment_sum(jnp.ones_like(flat_routes), flat_routes, num_segments...]
    all_to_all x1 -> x0, starting transfers between devices: 14.6 us -> none  [device_step(): lax.all_to_all(out_rows.reshape(local_experts, group_size, capacity, d_mo...]
    reduce_sum x2 -> x3, other arithmetic: 12.3 us -> 1.08 us  [the longest x1 0.88 us: route_plan(): picked = jnp.sum(jnp.where(hits, logits[:, None, :], 0.0), axis=2)]
  transfers between devices with their start and end apart: 1 -> 0, of which waited for: 1 -> 0; matrix products, arithmetic and copies ran while one was open for 7% -> 0% of each run, Pallas kernels for 0% -> 0%
where the time goes in v1:
time: 273 us
  Pallas kernels  260 us (95%)
  other arithmetic  7.27 us (3%)
  local copies, waits for them, and re-layouts  3.13 us (1%)
    pallas_call x1, Pallas kernels, device_step(): pl.pallas_call(functools.partial(moe_kernel, side, chunks, groups), out_s...  260 us

profile of v1, /device:TPU:0, one launch (start us, length us, event | category | flops | bytes accessed | tf_op | source)
XLA Modules:
  0.0 272.6 jit_solution(4921416260668567809)
XLA Ops:
  0.0 0.0 copy-start
  0.0 0.1 fusion.11
  0.1 0.9 compare_reduce_fusion
  1.0 0.2 convolution_select_fusion
  1.2 0.1 stack.9
  1.2 1.8 fusion.31
  3.0 0.0 copy-done
  3.0 0.1 copy.24
  3.2 0.9 select_reduce_fusion
  4.1 0.1 reduce_max.9
  4.2 0.1 copy.26
  4.3 0.2 fusion.1
  4.5 0.1 stack.10
  4.6 0.9 reshape.272.plans_hbm_0_
  5.5 0.9 reshape.273.plans_hbm_1_
  6.5 0.9 reshape.274.plans_hbm_2_
  7.4 260.1 %moe.1 = (f32[256,2048]{1,0:T(8,128)}, f32[3,256,2048]{2,1,0:T(8,128)}) custom-call(bf16[256,2048]{1,0:T(8,128)(2,1)} %tokens_hbm.1, f32[4,64,256]{2,1,0:T(8,128)} %reshape.272.plans_hbm_0_, f32[4,64,256]{2,1,0:T(8,128)} %reshape.273.plans_hbm_1_, f32[4,64,256]{2,1,0:T(8,128)} %reshape.274.plans_hbm_2_, bf16[2048,768]{1,0:T(8,128)(2,1)} %bitcast.27, ...), custom_call_target="tpu_custom_call" | custom-call | tf_op jit(solution)/shard_map/moe/pallas_call | solution.py:305
  267.5 5.1 %fusion = bf16[256,2048]{1,0:T(8,128)(2,1)} fusion(f32[256,2048]{1,0:T(8,128)} %get-tuple-element.7, f32[3,256,2048]{2,1,0:T(8,128)} %get-tuple-element.8), kind=kLoop, calls=%fused_computation.1 | loop fusion | flops 2097152 | bytes 9437184 | tf_op jit(solution)/shard_map/convert_element_type | solution.py:330
  (7 shorter events, 0.2 us)
Async XLA Ops:
  0.0 3.0 %copy-start = (s32[256,8]{0,1:T(8,128)S(1)}, s32[256,8]{0,1:T(8,128)}, u32[]{:S(2)}) copy-start(s32[256,8]{0,1:T(8,128)} %param.7) | copy-start | bytes 24580

commit v2 on v1

--- a/solution.py
+++ b/solution.py
@@ -37,27 +37,19 @@
     return ((digits[Z] * side + digits[Y]) * side + digits[X]) * 2 + (me + core_steps) % 2
 
 
-def route_plan(tokens, routes, w_router, expert_at):
-    num_tokens = tokens.shape[0]
-    num_experts = w_router.shape[1]
-    logits = jnp.dot(tokens, w_router, preferred_element_type=jnp.float32)
-    expert_ids = jnp.arange(num_experts, dtype=jnp.int32)
-    hits = routes[:, :, None] == expert_ids[None, None, :]
-    picked = jnp.sum(jnp.where(hits, logits[:, None, :], 0.0), axis=2)
-    gate_vals = jax.nn.softmax(picked, axis=-1)
-    routes_t = routes.T
-    gates_t = gate_vals.T
-    at = routes_t[:, None, :] == expert_at[None, :, None]
-    mask_t = jnp.any(at, axis=0)
-    gate_t = jnp.sum(jnp.where(at, gates_t[:, None, :], 0.0), axis=0)
-    token_ids = jnp.arange(num_tokens, dtype=jnp.int32)
-    before = (token_ids[:, None] < token_ids[None, :]).astype(jnp.bfloat16)
-    rank_t = jnp.dot(mask_t.astype(jnp.bfloat16), before, preferred_element_type=jnp.float32)
-    return jnp.where(mask_t, rank_t, -1.0), gate_t
-
-
-def moe_kernel(side, chunks, groups, tokens_hbm, plans_hbm, w_one_hbm, w_three_hbm, w_two_hbm, y_own, y_peers,
-               toks, plans, packed, relay, rows, w_one, w_three, w_two, parts,
+def expert_order(me, side, order, num_tokens):
+    bits = side.bit_length() - 1
+    position = lax.broadcasted_iota(jnp.int32, (2 * side ** 3, num_tokens), 0)
+    digits = [me // (2 * side * side), (me // (2 * side)) % side, (me // 2) % side]
+    for place, axis in enumerate(order):
+        steps = jnp.right_shift(position, 1 + (2 - place) * bits)
+        digits[axis] = jnp.bitwise_and(digits[axis] + steps, side - 1)
+    core = jnp.bitwise_and(me + position, 1)
+    return ((digits[Z] * side + digits[Y]) * side + digits[X]) * 2 + core
+
+
+def moe_kernel(side, chunks, groups, tokens_hbm, routes_ref, w_router, w_one_hbm, w_three_hbm, w_two_hbm, y_own, y_peers,
+               toks, plans, own_plans, packed, relay, rows, w_one, w_three, w_two, parts,
                load_sem, w_sem, s0_sem, r0_sem, sp_sem, rp_sem, s1_sem, r1_sem, s2_sem, r2_sem, b1_sem, c1_sem, b2_sem, c2_sem, s3_sem, r3_sem, out_sem, free2_sem, free3_sem):
     me = lax.axis_index('ep')
     dp = lax.axis_index('dp')
@@ -87,10 +79,11 @@
                  X: (q, slice(None), slice(None), c, core)}[third]
         return where + (slice(None), columns(g))
 
-    def gather_copies(g, a):
-        first = ORDERS[g][0]
-        return (remote(tokens_hbm.at[:, columns(g)], toks[g].at[a], s0_sem.at[g], r0_sem.at[g], first, a),
-                remote(plans_hbm[g].at[a], plans[g].at[a], sp_sem.at[g], rp_sem.at[g], first, a))
+    def gather_tokens(g, a):
+        return remote(tokens_hbm.at[:, columns(g)], toks[g].at[a], s0_sem.at[g], r0_sem.at[g], ORDERS[g][0], a)
+
+    def gather_plans(g, a):
+        return remote(own_plans[g].at[a], plans[g].at[a], sp_sem.at[g], rp_sem.at[g], ORDERS[g][0], a)
 
     def gather_all(g):
         first = ORDERS[g][0]
@@ -98,8 +91,11 @@
         return (remote(toks[g].at[others], toks[g].at[others], s0_sem.at[g], r0_sem.at[g], first, 1),
                 remote(plans[g].at[others], plans[g].at[others], sp_sem.at[g], rp_sem.at[g], first, 1))
 
-    def out_second(g, q, b):
-        return remote(packed[g].at[q, b], relay_from(g, q, b), s1_sem.at[g, q], r1_sem.at[g, q], ORDERS[g][1], b)
+    def relay_slab(g, q, a, b):
+        return relay[g].at[q, b, a] if g == 1 else relay[g].at[q, a, b]
+
+    def out_second(g, q, a, b):
+        return remote(packed[g].at[q, b, a], relay_slab(g, q, a, b), s1_sem.at[g, q], r1_sem.at[g, q], ORDERS[g][1], b)
 
     def out_second_all(g, q):
         return remote(packed[g].at[q, pl.ds(1, side - 1)], relay_others(g, q), s1_sem.at[g, q], r1_sem.at[g, q], ORDERS[g][1], 1)
@@ -129,53 +125,99 @@
     def tell(sem, axis, steps, core_steps=0):
         pl.semaphore_signal(sem, inc=1, device_id=(dp, moved(me, side, axis, steps, core_steps)), device_id_type=MESH)
 
-    loads = []
-    for g in range(3):
-        loads.append((pltpu.make_async_copy(tokens_hbm.at[:, columns(g)], toks[g].at[0], load_sem.at[2 * g]),
-                      pltpu.make_async_copy(plans_hbm[g].at[0], plans[g].at[0], load_sem.at[2 * g + 1])))
+    loads = [pltpu.make_async_copy(tokens_hbm.at[:, columns(g)], toks[g].at[0], load_sem.at[g]) for g in range(3)]
     weights = [pltpu.make_async_copy(src, dst, w_sem.at[i]) for i, (src, dst) in enumerate(
         [(w_one_hbm, w_one), (w_three_hbm, w_three), (w_two_hbm, w_two)])]
+    for copy in loads:
+        copy.start()
+
+    barrier = pltpu.get_barrier_semaphore()
+    tell(barrier, X, 0, 1)
+    for axis in (Z, Y, X):
+        for steps in range(1, side):
+            for core_steps in range(2):
+                tell(barrier, axis, steps, core_steps)
+    pl.semaphore_wait(barrier, 1 + 3 * (side - 1) * 2)
 
     for a in range(1, side):
         for g in range(3):
-            for copy in gather_copies(g, a)[::-1]:
-                copy.start()
+            gather_tokens(g, a).start()
+    for copy in loads:
+        copy.wait()
+
+    num_experts = 2 * side ** 3
+    logits = sum(jnp.dot(toks[g][0], w_router[columns(g), :], preferred_element_type=jnp.float32) for g in range(3)).T
+    ids = lax.broadcasted_iota(jnp.int32, (num_experts, num_tokens), 0)
+    top_k = routes_ref.shape[0]
+    picks = [routes_ref[k:k + 1, :] for k in range(top_k)]
+    scores = [jnp.sum(jnp.where(pick == ids, logits, 0.0), axis=0, keepdims=True) for pick in picks]
+    peak = functools.reduce(jnp.maximum, scores)
+    scores = [jnp.exp(score - peak) for score in scores]
+    norm = sum(scores)
+    gates = [score / norm for score in scores]
+    before = (lax.broadcasted_iota(jnp.int32, (num_tokens, num_tokens), 0)
+              < lax.broadcasted_iota(jnp.int32, (num_tokens, num_tokens), 1))
+    before = jnp.where(before, 1.0, 0.0).astype(jnp.bfloat16)
     for g in range(3):
-        for copy in loads[g]:
-            copy.start()
+        expert_at = expert_order(me, side, ORDERS[g], num_tokens)
+        mask = jnp.zeros((num_experts, num_tokens), jnp.float32)
+        gate = jnp.zeros((num_experts, num_tokens), jnp.float32)
+        for k in range(top_k):
+            hit = picks[k] == expert_at
+            mask = jnp.where(hit, 1.0, mask)
+            gate = jnp.where(hit, gates[k], gate)
+        slot = jnp.dot(mask.astype(jnp.bfloat16), before, preferred_element_type=jnp.float32)
+        slot = jnp.where(mask > 0.0, slot, -1.0)
+        plans[g][0, pl.ds(0, plane), :] = slot[:plane]
+        plans[g][0, pl.ds(plane, plane), :] = gate[:plane]
+        for a in range(1, side):
+            own_plans[g][a, pl.ds(0, plane), :] = slot[a * plane:(a + 1) * plane]
+            own_plans[g][a, pl.ds(plane, plane), :] = gate[a * plane:(a + 1) * plane]
+        for a in range(1, side):
+            gather_plans(g, a).start()
     for copy in weights:
         copy.start()
-    parts[...] = jnp.zeros_like(parts)
 
     def taken(g, q, a):
         slots = plans[g][a, pl.ds(0, plane), :]
         ids = lax.broadcasted_iota(jnp.int32, (plane, SLOTS, num_tokens), 1) + q * SLOTS
         return jnp.broadcast_to(slots[:, None, :], (plane, SLOTS, num_tokens)) == ids.astype(jnp.float32)
 
+    def pack(g, q, a):
+        select = jnp.where(taken(g, q, a), 1.0, 0.0).reshape(packed_rows, num_tokens).astype(jnp.bfloat16)
+        out = jnp.dot(select, toks[g][a], preferred_element_type=jnp.float32)
+        out = out.reshape(side, ends, SLOTS, groups[g][1]).astype(jnp.bfloat16)
+        packed[g][q, pl.ds(1, side - 1), a] = out[1:]
+        for b in range(1, side):
+            out_second(g, q, a, b).start()
+        relay_slab(g, q, a, 0)[...] = out[0]
+
+    def pack_own(q, carry):
+        for g in range(3):
+            pack(g, q, 0)
+        return carry
+
+    lax.fori_loop(0, chunks, pack_own, 0)
+    parts[...] = jnp.zeros_like(parts)
     for g in range(3):
-        for copy in loads[g]:
-            copy.wait()
         for copy in gather_all(g):
             copy.wait_recv()
 
-    def pack(q, carry):
-        for g in range(3):
-            width = groups[g][1]
-
-            def source(a, c):
-                select = jnp.where(taken(g, q, a), 1.0, 0.0).reshape(packed_rows, num_tokens).astype(jnp.bfloat16)
-                out = jnp.dot(select, toks[g][a], preferred_element_type=jnp.float32)
-                packed[g][q, :, a] = out.reshape(side, ends, SLOTS, width).astype(jnp.bfloat16)
-                return c
-            lax.fori_loop(0, side, source, 0)
-            for b in range(1, side):
-                out_second(g, q, b).start()
-            relay_from(g, q, 0)[...] = packed[g][q, 0]
+    def outward(i, carry):
+        @pl.when(i < chunks)
+        def _():
+            for g in range(3):
+                def source(a, c):
+                    pack(g, i, a)
+                    return c
+                lax.fori_loop(1, side, source, 0)
+
+        @pl.when(i > 0)
+        def _():
+            forward(i - 1)
         return carry
 
-    lax.fori_loop(0, chunks, pack, 0)
-
-    def forward(q, carry):
+    def forward(q):
         for g in range(3):
             out_second_all(g, q).wait_recv()
             for e in range(1, ends):
@@ -184,9 +226,8 @@
             out_second_all(g, q).wait_send()
             for b in range(1, side):
                 tell(free2_sem.at[g, q], ORDERS[g][1], b)
-        return carry
-
-    lax.fori_loop(0, chunks, forward, 0)
+
+    lax.fori_loop(0, chunks + 1, outward, 0)
     for copy in weights:
         copy.wait()
 
@@ -217,23 +258,21 @@
 
     lax.fori_loop(0, chunks, experts, 0)
 
-    def backward(q, carry):
+    def backward(q):
         for g in range(3):
             third_all(g, q, b1_sem, c1_sem).wait_recv()
             pl.semaphore_wait(free2_sem.at[g, q], side - 1)
             for b in range(1, side):
                 home_second(g, q, b).start()
             packed[g][q, 0] = relay_from(g, q, 0)[...]
-        return carry
-
-    lax.fori_loop(0, chunks, backward, 0)
-
-    def combine(q, carry):
-        for g in range(3):
+
+    def combine(q):
+        for g in (1, 2, 0):
             home_second_all(g, q).wait_recv()
             width = groups[g][1]
 
-            def source(a, c):
+            def source(i, c):
+                a = (i + 1) % side
                 gates = plans[g][a, pl.ds(plane, plane), :]
                 used = taken(g, q, a)
                 o = packed[g][q, :, a].astype(jnp.float32).reshape(packed_rows, width).astype(jnp.bfloat16)
@@ -245,16 +284,24 @@
                     term = lax.dot_general(mix, o, (((0,), (0,)), ((), ())), preferred_element_type=jnp.float32)
                     total = term if total is None else total + term
                 parts[a, :, columns(g)] += total
+
+                @pl.when(jnp.logical_and(q == chunks - 1, a > 0))
+                def _():
+                    home_first(g, a).start()
                 return c
             lax.fori_loop(0, side, source, 0)
 
-            @pl.when(q == chunks - 1)
-            def _():
-                for a in range(1, side):
-                    home_first(g, a).start()
+    def homeward(i, carry):
+        @pl.when(i < chunks)
+        def _():
+            backward(i)
+
+        @pl.when(i > 0)
+        def _():
+            combine(i - 1)
         return carry
 
-    lax.fori_loop(0, chunks, combine, 0)
+    lax.fori_loop(0, chunks + 1, homeward, 0)
     own = pltpu.make_async_copy(parts.at[0], y_own, out_sem)
     own.start()
 
@@ -287,18 +334,8 @@
         chunks = capacity // SLOTS
         groups = column_groups(d_model)
         plane = 2 * side * side
-        me = lax.axis_index('ep')
-        position = jnp.arange(num_experts, dtype=jnp.int32)
-        expert_at = moved(me, side, Z, position // plane)
-        expert_at = moved(expert_at, side, Y, (position // (2 * side)) % side)
-        expert_at = moved(expert_at, side, X, (position // 2) % side, position % 2)
-        slot_t, gate_t = route_plan(tokens, routes, w_router, expert_at)
-        plan = jnp.stack([slot_t, gate_t]).reshape(2, side, side, side, 2, num_tokens)
-        plans = []
-        for first, second, third in ORDERS:
-            ordered = jnp.transpose(plan, (1 + first, 0, 1 + second, 1 + third, 4, 5))
-            plans.append(ordered.reshape(side, 2 * plane, num_tokens))
         hbm = pl.BlockSpec(memory_space=pl.ANY)
+        vmem = pl.BlockSpec(memory_space=pltpu.VMEM)
         dma = pltpu.SemaphoreType.DMA
         slab = [[pltpu.VMEM((chunks, side, side, 2 * side, SLOTS, width), jnp.bfloat16) for _, width in groups] for _ in range(2)]
         pair = [dma((3, chunks)), dma((3, chunks))]
@@ -306,10 +343,11 @@
             functools.partial(moe_kernel, side, chunks, groups),
             out_shape=(jax.ShapeDtypeStruct((num_tokens, d_model), jnp.float32),
                        jax.ShapeDtypeStruct((side - 1, num_tokens, d_model), jnp.float32)),
-            in_specs=[hbm, (hbm, hbm, hbm), hbm, hbm, hbm],
+            in_specs=[hbm, vmem, vmem, hbm, hbm, hbm],
             out_specs=(hbm, hbm),
             scratch_shapes=[
                 [pltpu.VMEM((side, num_tokens, width), jnp.bfloat16) for _, width in groups],
+                [pltpu.VMEM((side, 2 * plane, num_tokens), jnp.float32) for _ in groups],
                 [pltpu.VMEM((side, 2 * plane, num_tokens), jnp.float32) for _ in groups],
                 slab[0], slab[1],
                 pltpu.VMEM((chunks, side, side, side, 2, SLOTS, d_model), jnp.bfloat16),
@@ -317,13 +355,13 @@
                 pltpu.VMEM((d_model, d_expert), jnp.bfloat16),
                 pltpu.VMEM((d_expert, d_model), jnp.bfloat16),
                 pltpu.VMEM((side, num_tokens, d_model), jnp.float32),
-                dma((6,)), dma((3,)), dma((3,)), dma((3,)), dma((3,)), dma((3,)),
+                dma((3,)), dma((3,)), dma((3,)), dma((3,)), dma((3,)), dma((3,)),
                 *pair, *pair, *pair, *pair, dma((3,)), dma((3,)), dma,
                 pltpu.SemaphoreType.REGULAR((3, chunks)), pltpu.SemaphoreType.REGULAR((3, chunks)),
             ],
-            compiler_params=pltpu.CompilerParams(has_side_effects=True, vmem_limit_bytes=67043328),
+            compiler_params=pltpu.CompilerParams(collective_id=0, has_side_effects=True, vmem_limit_bytes=67043328),
             name='moe',
-        )(tokens, tuple(plans), w_one[0], w_three[0], w_two[0])
+        )(tokens, routes.T, w_router, w_one[0], w_three[0], w_two[0])
         total = y_own
         for i in range(side - 1):
             total = total + y_peers[i]

time: 273 us -> 258 us (0.945)
  Pallas kernels: 260 us -> 253 us
  local copies, waits for them, and re-layouts: 3.13 us -> 0 us
    pallas_call x1, Pallas kernels: 260 us -> 253 us  [device_step(): pl.pallas_call(functools.partial(moe_kernel, side, chunks, groups), out_s...]
where the time goes in v2:
time: 258 us
  Pallas kernels  253 us (98%)
  other arithmetic  5.11 us (2%)
    pallas_call x1, Pallas kernels, device_step(): pl.pallas_call(functools.partial(moe_kernel, side, chunks, groups), out_s...  253 us

profile of v2, /device:TPU:0, one launch (start us, length us, event | category | flops | bytes accessed | tf_op | source)
XLA Modules:
  0.0 257.9 jit_solution(7834180656339198728)
XLA Ops:
  0.0 252.8 %moe.1 = (f32[256,2048]{1,0:T(8,128)}, f32[3,256,2048]{2,1,0:T(8,128)}) custom-call(bf16[256,2048]{1,0:T(8,128)(2,1)} %tokens_hbm.1, s32[8,256]{1,0:T(8,128)} %bitcast.19, bf16[2048,128]{1,0:T(8,128)(2,1)} %w_router.1, bf16[2048,768]{1,0:T(8,128)(2,1)} %bitcast.16, bf16[2048,768]{1,0:T(8,128)(2,1)} %bitcast.17, bf16[768,2048]{1,0:T(8,128)(2,1)} %bitcast.18), custom_call_target="tpu_custom_call" | custom-call | tf_op jit(solution)/shard_map/moe/pallas_call | solution.py:342
  252.8 5.1 %fusion = bf16[256,2048]{1,0:T(8,128)(2,1)} fusion(f32[256,2048]{1,0:T(8,128)} %get-tuple-element.7, f32[3,256,2048]{2,1,0:T(8,128)} %get-tuple-element.8), kind=kLoop, calls=%fused_computation.1 | loop fusion | flops 2097152 | bytes 9437184 | tf_op jit(solution)/shard_map/convert_element_type | solution.py:368
